TPU v7x, 32 devices: a whole 2x2x4 slice. The times are simulated.
32 devices in a mesh: dp: 16 (over z, x, core), mp: 2 (over y).
Axes of the slice: x: 2, y: 2, z: 4, core: 2. Of those that a mesh axis runs over, the one named last changes fastest.
Arguments:
- ranges: bfloat16 [512, 2652], P(('dp', 'mp')), may hold values from 0.0099487305 to 1
- board: int32 [512, 5], P(('dp', 'mp')), may hold values from 0 to 51, as said below
- targets: bfloat16 [512, 2652], P(('dp', 'mp')), may hold values from -6 to 6
- w_in: bfloat16 [1536, 2704], P(('mp', 'dp')), may hold values from -0.34570312 to 0.34570312
- w_out: bfloat16 [1536, 2652], P(('mp', 'dp')), may hold values from -0.3046875 to 0.3046875
Outputs:
- predicted: bfloat16 [512, 2652], P(('dp', 'mp'))
- update_in: float32 [1536, 2704], P(('mp', 'dp'))
- update_out: float32 [1536, 2652], P(('mp', 'dp'))
- loss: float32 [], replicated
Inputs may be any that keep to these rules, and one draw needn't show every extreme that they name: `board`: each row holds 5 different cards.
All inputs are finite; a program needn't handle non-finite values.
Results may differ from a plain program's by a relative error of at most 0.014.
Values may be sent and summed in bfloat16 or wider, within the bound.
A program may use at most 64 MiB of HBM per device.

v0:
```python
import jax
import jax.numpy as jnp
from jax import lax
from jax.sharding import PartitionSpec as P

CARDS = 52
HIDDEN_SIZE = 1536


def huber_terms(error_value):
    magnitude = jnp.abs(error_value)
    return jnp.where(magnitude <= 1.0, 0.5 * error_value * error_value, magnitude - 0.5)


def build_features(all_ranges, all_board, card_count):
    card_ids = jnp.arange(card_count, dtype=jnp.int32)
    onehot_board = jnp.sum(
        (all_board[:, :, None] == card_ids[None, None, :]).astype(jnp.float32), axis=1
    ).astype(jnp.bfloat16)
    return jnp.concatenate([all_ranges, onehot_board], axis=1)


def right_product(left_side, right_block):
    return lax.dot_general(
        left_side, right_block, (((1,), (1,)), ((), ())), preferred_element_type=jnp.float32
    )


def left_product(left_side, right_side):
    return lax.dot_general(
        left_side, right_side, (((0,), (0,)), ((), ())), preferred_element_type=jnp.float32
    )


def body(ranges, board, targets, w_in, w_out):
    mp_count = lax.axis_size("mp")
    dp_count = lax.axis_size("dp")
    stored_rows = ranges.shape[0]
    value_width = w_out.shape[1]
    all_ranges, all_board = (
        lax.all_gather(ranges, "mp", axis=0, tiled=True),
        lax.all_gather(board, "mp", axis=0, tiled=True),
    )
    features = build_features(all_ranges, all_board, CARDS)
    local_in = lax.all_gather(w_in, "dp", axis=0, tiled=True)
    preact = right_product(features, local_in)
    hidden = jax.nn.gelu(preact).astype(jnp.bfloat16)
    local_out = lax.all_gather(w_out, "dp", axis=0, tiled=True)
    partial_value = jnp.dot(hidden, local_out, preferred_element_type=jnp.float32)
    stacked = partial_value.astype(jnp.bfloat16).reshape(mp_count, stored_rows, value_width)
    received = lax.all_to_all(stacked, "mp", split_axis=0, concat_axis=0, tiled=True)
    summed = jnp.sum(received.astype(jnp.float32), axis=0)
    error_value = summed - targets.astype(jnp.float32)
    own_grad = jnp.clip(error_value, -1.0, 1.0).astype(jnp.bfloat16)
    out_grad = lax.all_gather(own_grad, "mp", axis=0, tiled=True)
    predicted = summed.astype(jnp.bfloat16)
    loss_part = jnp.sum(huber_terms(error_value))
    loss_total = lax.psum(loss_part, ("dp", "mp"))
    grad_out = lax.psum_scatter(
        left_product(hidden, out_grad), "dp", scatter_dimension=0, tiled=True
    )
    back_out = lax.all_gather(w_out, "dp", axis=0, tiled=True)
    hidden_grad = right_product(out_grad, back_out)
    unused_value, gelu_back = jax.vjp(jax.nn.gelu, preact)
    preact_grad = gelu_back(hidden_grad)[0].astype(jnp.bfloat16)
    grad_in = lax.psum_scatter(
        left_product(preact_grad, features), "dp", scatter_dimension=0, tiled=True
    )
    square_part = jnp.sum(grad_in * grad_in) + jnp.sum(grad_out * grad_out)
    square_total = lax.psum(square_part, ("dp", "mp"))
    count_params = HIDDEN_SIZE * (w_in.shape[1] + value_width)
    scale = lax.rsqrt(square_total / count_params + 1e-06)
    loss = loss_total / (stored_rows * mp_count * dp_count * value_width)
    return (predicted, grad_in * scale, grad_out * scale, loss)


def solution(mesh):
    in_specs = (
        P(("dp", "mp"), None),
        P(("dp", "mp"), None),
        P(("dp", "mp"), None),
        P(("mp", "dp"), None),
        P(("mp", "dp"), None),
    )
    out_specs = (P(("dp", "mp"), None), P(("mp", "dp"), None), P(("mp", "dp"), None), P())
    return jax.shard_map(body, mesh=mesh, in_specs=in_specs, out_specs=out_specs, check_vma=False)
```

profile of v0, /device:TPU:0, one launch (start us, length us, event | category | flops | bytes accessed | tf_op | source)
XLA Modules:
  0.0 402.8 jit_solution(9901448083366208325)
XLA Ops:
  7.2 0.0 all-gather.4.cloned.1.call-start
  7.2 0.7 all-gather.4.cloned.1.call-update
  7.9 0.0 all-gather.6.cloned.1.call-start
  7.9 0.7 all-gather.6.cloned.1.call-update
  8.6 0.0 reduce-scatter.5.cloned.1.call-start
  8.7 5.5 %all-gather = s32[2,16,5]{1,2,0:T(8,128)S(1)} all-gather(s32[1,16,5]{1,2,0:T(8,128)} %bitcast.10), channel_id=1, replica_groups=mesh['dp'=16,'mp'=2] {'mp'}, dimensions={0}, use_global_device_ids=true | all-gather | bytes 960 | tf_op jit(solution)/shard_map/all_gather | solution.py:42
  14.2 0.1 reshape.14
  14.3 5.4 %all_gather.16 = bf16[32,2652]{1,0:T(8,128)(2,1)S(1)} all-gather(bf16[16,2652]{1,0:T(8,128)(2,1)} %param.5), channel_id=1, replica_groups=mesh['dp'=16,'mp'=2] {'mp'}, dimensions={0}, use_global_device_ids=true | all-gather | bytes 254592 | tf_op jit(solution)/shard_map/all_gather | solution.py:41
  19.7 0.1 convert_reduce_fusion.1
  19.7 0.0 copy-start
  19.8 44.3 %all-gather.4.cloned.1.call-done = bf16[768,2704]{1,0:T(8,128)(2,1)} async-done(((bf16[48,2704]{1,0:T(8,128)(2,1)}), bf16[768,2704]{1,0:T(8,128)(2,1)}) %all-gather.4.cloned.1.call-update) | async-done | bytes 4153360 | tf_op jit(solution)/shard_map/all_gather | solution.py:45
  64.1 3.6 fusion.3
  67.6 47.4 %all-gather.6.cloned.1.call-done = bf16[768,2652]{1,0:T(8,128)(2,1)} async-done(((bf16[48,2652]{1,0:T(8,128)(2,1)}), bf16[768,2652]{1,0:T(8,128)(2,1)}) %all-gather.6.cloned.1.call-update) | async-done | bytes 4073488 | tf_op jit(solution)/shard_map/all_gather | solution.py:48
  115.1 3.0 convolution_convert_fusion
  118.0 7.2 %all_to_all.5 = bf16[2,16,2652]{2,1,0:T(8,128)(2,1)S(1)} all-to-all(bf16[2,16,2652]{2,1,0:T(8,128)(2,1)S(1)} %bitcast.9), channel_id=1, replica_groups=mesh['dp'=16,'mp'=2] {'mp'}, dimensions={0} | all-to-all | bytes 339456 | tf_op jit(solution)/shard_map/all_to_all | solution.py:51
  125.3 0.0 copy-done
  125.3 1.3 fusion.1
  126.6 5.1 %all_gather.20 = bf16[32,2652]{1,0:T(8,128)(2,1)S(1)} all-gather(bf16[16,2652]{1,0:T(8,128)(2,1)S(1)} %get-tuple-element.7), channel_id=1, replica_groups=mesh['dp'=16,'mp'=2] {'mp'}, dimensions={0}, use_global_device_ids=true | all-gather | bytes 254592 | tf_op jit(solution)/shard_map/all_gather | solution.py:55
  131.8 4.5 %fusion.26 = f32[768,2652]{1,0:T(8,128)} fusion(bf16[32,2652]{1,0:T(8,128)(2,1)S(1)} %all_gather.20, f32[32,768]{1,0:T(8,128)S(1)} %fusion.3), kind=kOutput, calls=%fused_computation.40 | convolution fusion | flops 130572288 | bytes 8414976 | tf_op jit(solution)/shard_map/dot_general | solution.py:30
  136.2 0.0 reduce-scatter.5.cloned.1.call-update
  136.2 0.0 reduce-scatter.3.cloned.1.call-start
  136.3 9.1 %fusion.2 = f32[768,2704]{1,0:T(8,128)} fusion(bf16[32,52]{1,0:T(8,128)(2,1)S(1)} %convert_reduce_fusion.1, bf16[32,2652]{1,0:T(8,128)(2,1)S(1)} %all_gather.16, f32[32,768]{1,0:T(8,128)S(1)} %fusion.3, bf16[32,2652]{1,0:T(8,128)(2,1)S(1)} %all_gather.20, bf16[768,2652]{1,0:T(8,128)(2,1)} %all-gather.6.cloned.1.call-done), kind=kOutput, calls=%fused_computation.14 | convolution fusion | flops 264095744 | bytes 12821248 | tf_op jit(solution)/shard_map/dot_general | solution.py:30
  145.4 0.0 reduce-scatter.3.cloned.1.call-update
  145.5 91.6 %reduce-scatter.5.cloned.1.call-done = f32[48,2652]{1,0:T(8,128)} async-done(((f32[768,2652]{1,0:T(8,128)}), f32[48,2652]{1,0:T(8,128)}) %reduce-scatter.5.cloned.1.call-update) | async-done | bytes 509200 | tf_op jit(solution)/shard_map/reduce_scatter | solution.py:59
  237.0 1.8 multiply_reduce_fusion.1
  238.8 107.6 %reduce-scatter.3.cloned.1.call-done = f32[48,2704]{1,0:T(8,128)} async-done(((f32[768,2704]{1,0:T(8,128)}), f32[48,2704]{1,0:T(8,128)}) %reduce-scatter.3.cloned.1.call-update) | async-done | bytes 519184 | tf_op jit(solution)/shard_map/reduce_scatter | solution.py:66
  346.4 1.8 multiply_reduce_fusion
  349.5 40.5 %all-reduce = (f32[]{:T(128)}, f32[]{:T(128)}) all-reduce(f32[]{:T(128)S(6)} %add.26, f32[]{:T(128)} %get-tuple-element.6), channel_id=1, replica_groups=mesh['dp'=16,'mp'=2] {'dp','mp'}, use_global_device_ids=true, to_apply=%region_6.7 | all-reduce | flops 2 | bytes 16 | tf_op jit(solution)/shard_map/psum | solution.py:70
  391.4 1.9 broadcast_multiply_fusion.1
  393.3 1.9 broadcast_multiply_fusion
  (2 shorter events, 0.0 us)
Async XLA Ops:
  7.2 56.9 %all-gather.4.cloned.1.call-start = ((), (), s32[]{:S(2)}) async-start(), calls=%async_computation.3 | async-start | bytes 4595712 | tf_op jit(solution)/shard_map/all_gather | solution.py:45
  7.9 107.2 %all-gather.6.cloned.1.call-start = ((), (), s32[]{:S(2)}) async-start(), calls=%async_computation.4 | async-start | bytes 4386816 | tf_op jit(solution)/shard_map/all_gather | solution.py:48
  8.6 228.4 %reduce-scatter.5.cloned.1.call-start = ((), (), s32[]{:S(2)}) async-start(), calls=%async_computation.6 | async-start | bytes 8773632 | tf_op jit(solution)/shard_map/reduce_scatter | solution.py:59
  19.7 105.6 %copy-start = (bf16[16,2652]{1,0:T(8,128)(2,1)S(1)}, bf16[16,2652]{1,0:T(8,128)(2,1)}, u32[]{:S(2)}) copy-start(bf16[16,2652]{1,0:T(8,128)(2,1)} %param.7) | copy-start | bytes 254596
  136.2 210.2 %reduce-scatter.3.cloned.1.call-start = ((), (), s32[]{:S(2)}) async-start(), calls=%async_computation.5 | async-start | bytes 9191424 | tf_op jit(solution)/shard_map/reduce_scatter | solution.py:66
Sparse Core Ops, SparseCore 0:
  10.3 53.7 all-gather.3
  66.4 48.6 all-gather.5
  136.4 100.6 reduce-scatter.4
  241.0 105.4 reduce-scatter.2
where the time goes:
time: 403 us
  waiting for transfers between devices  292 us (72%)
  blocking collectives  63.8 us (16%)
  matrix products  20.1 us (5%)
  between operations  17.6 us (4%)
  other arithmetic  8.71 us (2%)
    reduce_scatter x1, waiting for transfers between devices, body(): lax.psum_scatter(left_product(preact_grad, features), 'dp', scatter_dimen...  108 us
    reduce_scatter x1, waiting for transfers between devices, body(): lax.psum_scatter(left_product(hidden, out_grad), 'dp', scatter_dimension=...  91.6 us
    all_gather x1, waiting for transfers between devices, body(): local_out = lax.all_gather(w_out, 'dp', axis=0, tiled=True)  47.4 us
    all_gather x1, waiting for transfers between devices, body(): local_in = lax.all_gather(w_in, 'dp', axis=0, tiled=True)  44.3 us
    psum x1, blocking collectives, body(): square_total = lax.psum(square_part, ('dp', 'mp'))  40.5 us
    dot_general x2, matrix products, left_product(): lax.dot_general(left_side, right_side, (((0,), (0,)), ((), ())), preferre...  13.6 us
  transfers between devices with their start and end apart: 4, of which 4 were waited for; matrix products, arithmetic and copies ran while one was open for 4% of the time, Pallas kernels for 0%

commit v1 on v0

v1 whole, which is shorter than its diff:
```python
import functools

import jax
import jax.numpy as jnp
from jax import lax
from jax.experimental import pallas as pl
from jax.experimental.pallas import tpu as pltpu
from jax.sharding import PartitionSpec as P

CARDS = 52
MESH = pl.DeviceIdType.MESH
GELU_K = 0.7978845608028654
GELU_C = 0.044715


def huber_terms(error_value):
    magnitude = jnp.abs(error_value)
    return jnp.where(magnitude <= 1.0, 0.5 * error_value * error_value, magnitude - 0.5)


def dot_nt(a, b):
    return lax.dot_general(a, b, (((1,), (1,)), ((), ())), preferred_element_type=jnp.float32)


def dot_nn(a, b):
    return lax.dot_general(a, b, (((1,), (0,)), ((), ())), preferred_element_type=jnp.float32)


def column_chunks(width, count):
    tiles = -(-width // 128)
    edges = [min(width, 128 * (-(-tiles * k // count))) for k in range(count + 1)]
    return [pl.ds(a, b - a) for a, b in zip(edges[:-1], edges[1:]) if b > a]


def step_kernel(
    dp, mp, chunks,
    feat_ref, targets_ref, w_in_ref, w_out_ref,
    pred_ref, gin_ref, gout_ref, stat_ref,
    feats, ogs, og_own, win, wout, preact, hidden, partial,
    sp, lp, sr, rr, sl, rl, sgo, lgo, sgi, lgi,
    w_sem, ag1, ag2, p_sem, r_sem, l_sem, g_sem,
):
    chips = dp // 2
    n_right, n_left = chips // 2, (chips - 1) // 2
    rows = feat_ref.shape[0]
    units = w_in_ref.shape[0]
    me = lax.axis_index("dp")
    me_mp = lax.axis_index("mp")
    core = me % 2
    chip = me // 2
    odd = chip % 2
    pos = (1 - odd) * (chip // 2) + odd * (chips - 1 - chip // 2)

    def dp_at(rel, core_index):
        there = (pos + rel + chips) % chips
        half = there // (chips // 2)
        where = (1 - half) * (2 * there) + half * (2 * (chips - 1 - there) + 1)
        return where * 2 + core_index

    right = (dp_at(1, core), me_mp)
    left = (dp_at(-1, core), me_mp)
    partner = (chip * 2 + 1 - core, me_mp)
    peers = [(me, (me_mp + j) % mp) for j in range(1, mp)]
    back_peers = [(me, (me_mp - j + mp) % mp) for j in range(1, mp)]

    barrier = pltpu.get_barrier_semaphore()
    greeted = [right, left, partner] + peers
    for other in greeted:
        pl.semaphore_signal(barrier, inc=1, device_id=other, device_id_type=MESH)
    pl.semaphore_wait(barrier, len(greeted))

    def block(rel, core_index):
        return pl.ds(pl.multiple_of(dp_at(rel, core_index) * rows, rows), rows)

    def send(src, dst, sems, index, device):
        copy = pltpu.make_async_remote_copy(
            src_ref=src, dst_ref=dst,
            send_sem=sems.at[(0,) + index], recv_sem=sems.at[(1,) + index],
            device_id=device, device_id_type=MESH,
        )
        copy.start()
        return copy

    def start_gather(own_ref, buf, sems):
        pieces = column_chunks(buf.shape[1], chunks)
        here = block(0, core)
        first = {}
        for k, piece in enumerate(pieces):
            first["r", k] = send(own_ref.at[:, piece], buf.at[here, piece], sems, (0, 0, k), right)
            first["l", k] = send(own_ref.at[:, piece], buf.at[here, piece], sems, (1, 0, k), left)
        first["p"] = [
            send(own_ref.at[:, piece], buf.at[here, piece], sems, (2, 0, k), partner)
            for k, piece in enumerate(pieces)
        ]
        return first

    def finish_gather(own_ref, buf, sems, first):
        pieces = column_chunks(buf.shape[1], chunks)
        here = block(0, core)
        buf[here, :] = own_ref[...]
        flying = {k: v for k, v in first.items() if k != "p"}
        done = []
        partner_copies = list(first["p"])
        count = 1
        for s in range(n_right):
            coming = {}
            for side, steps, sign, lane, device in (
                ("r", n_right, -1, 0, right), ("l", n_left, 1, 1, left)
            ):
                if s >= steps:
                    continue
                spot = block(sign * (s + 1), core)
                for k, piece in enumerate(pieces):
                    copy = flying[side, k]
                    copy.wait_recv()
                    done.append(copy)
                    part = buf.at[spot, piece]
                    if s + 1 < steps:
                        coming[side, k] = send(part, part, sems, (lane, s + 1, k), device)
                    partner_copies.append(send(part, part, sems, (2, count, k), partner))
                count += 1
            flying = coming
        for copy in partner_copies:
            copy.wait_recv()
        for copy in done + partner_copies:
            copy.wait_send()

    first = start_gather(feat_ref, feats, ag1)
    weight_copies = []
    for j, device in enumerate(back_peers):
        weight_copies.append(send(w_in_ref, win.at[j + 1], w_sem, (0, j), device))
        weight_copies.append(send(w_out_ref, wout.at[j + 1], w_sem, (1, j), device))
    win[0] = w_in_ref[...]
    wout[0] = w_out_ref[...]
    finish_gather(feat_ref, feats, ag1, first)
    for copy in weight_copies:
        copy.wait()

    all_units = mp * units
    win_all = win[...].reshape(all_units, win.shape[2])
    pre = dot_nt(feats[...], win_all)
    preact[...] = pre
    tanh_value = jnp.tanh(GELU_K * (pre + GELU_C * pre * pre * pre))
    hidden_value = 0.5 * pre * (1.0 + tanh_value)
    hidden[...] = hidden_value.astype(jnp.bfloat16)
    partial[...] = dot_nn(hidden[...], wout[...].reshape(all_units, wout.shape[2]))

    order = []
    for s in range(n_right):
        order.append(n_right - s)
        if s < n_left:
            order.append(-(n_left - s))
    order.append(0)
    shared = {}
    for k, rel in enumerate(order):
        sp[k] = partial[block(rel, 1 - core), :].astype(jnp.bfloat16)
        shared[rel] = (k, send(sp.at[k], lp.at[k], p_sem, (k,), partner))

    def contribution(rel):
        k, copy = shared[rel]
        copy.wait_recv()
        return partial[block(rel, core), :] + lp[k].astype(jnp.float32)

    right_copies, left_copies = [], []
    for s in range(n_right):
        total = contribution(n_right - s)
        if s:
            right_copies[-1].wait_recv()
            total = total + rr[s - 1].astype(jnp.float32)
        sr[s] = total.astype(jnp.bfloat16)
        right_copies.append(send(sr.at[s], rr.at[s], r_sem, (s,), right))
        if s < n_left:
            total = contribution(-(n_left - s))
            if s:
                left_copies[-1].wait_recv()
                total = total + rl[s - 1].astype(jnp.float32)
            sl[s] = total.astype(jnp.bfloat16)
            left_copies.append(send(sl.at[s], rl.at[s], l_sem, (s,), left))
    summed = contribution(0)
    right_copies[-1].wait_recv()
    summed = summed + rr[n_right - 1].astype(jnp.float32)
    left_copies[-1].wait_recv()
    summed = summed + rl[n_left - 1].astype(jnp.float32)

    error_value = summed - targets_ref[...].astype(jnp.float32)
    og_own[...] = jnp.clip(error_value, -1.0, 1.0).astype(jnp.bfloat16)
    first = start_gather(og_own, ogs, ag2)
    pred_ref[...] = summed.astype(jnp.bfloat16)
    loss_part = jnp.sum(huber_terms(error_value))
    pre = preact[...]
    tanh_value = jnp.tanh(GELU_K * (pre + GELU_C * pre * pre * pre))
    slope = 0.5 * (1.0 + tanh_value) + 0.5 * pre * (1.0 - tanh_value * tanh_value) * (
        GELU_K * (1.0 + 3.0 * GELU_C * pre * pre)
    )
    hidden_t = jnp.transpose(hidden[...].astype(jnp.float32)).astype(jnp.bfloat16)
    for _, copy in shared.values():
        copy.wait_send()
    for copy in right_copies + left_copies:
        copy.wait_send()
    finish_gather(og_own, ogs, ag2, first)

    grad_copies = []
    go = dot_nn(hidden_t, ogs[...])
    for j, device in enumerate(peers):
        sgo[j] = go[(j + 1) * units:(j + 2) * units, :].astype(jnp.bfloat16)
        grad_copies.append(send(sgo.at[j], lgo.at[j], g_sem, (0, j), device))
    gout_ref[...] = go[:units, :]
    hidden_grad = dot_nt(ogs[...], wout[...].reshape(all_units, wout.shape[2]))
    preact_grad = jnp.transpose(hidden_grad * slope).astype(jnp.bfloat16)
    gi = dot_nn(preact_grad, feats[...])
    for j, device in enumerate(peers):
        sgi[j] = gi[(j + 1) * units:(j + 2) * units, :].astype(jnp.bfloat16)
        grad_copies.append(send(sgi.at[j], lgi.at[j], g_sem, (1, j), device))
    gin_ref[...] = gi[:units, :]
    for copy in grad_copies:
        copy.wait()
    go_own = gout_ref[...]
    gi_own = gin_ref[...]
    for j in range(mp - 1):
        go_own = go_own + lgo[j].astype(jnp.float32)
        gi_own = gi_own + lgi[j].astype(jnp.float32)
    gout_ref[...] = go_own
    gin_ref[...] = gi_own
    squares = jnp.sum(gi_own * gi_own) + jnp.sum(go_own * go_own)
    row = lax.broadcasted_iota(jnp.int32, stat_ref.shape, 0)
    stat_ref[...] = jnp.where(row == 0, loss_part, squares)


def body(ranges, board, targets, w_in, w_out):
    mp = lax.axis_size("mp")
    dp = lax.axis_size("dp")
    rows, out_w = targets.shape
    units_real, in_w = w_in.shape
    pad = -units_real % 16
    if pad:
        w_in = jnp.pad(w_in, ((0, pad), (0, 0)))
        w_out = jnp.pad(w_out, ((0, pad), (0, 0)))
    units = units_real + pad
    card_ids = jnp.arange(CARDS, dtype=jnp.int32)
    onehot = jnp.any(board[:, :, None] == card_ids[None, None, :], axis=1).astype(jnp.bfloat16)
    features = jnp.concatenate([ranges, onehot], axis=1)

    chips = dp // 2
    n_right, n_left = chips // 2, (chips - 1) // 2
    chunks = 2
    batch = dp * rows
    all_units = mp * units
    bf16, f32 = jnp.bfloat16, jnp.float32
    vmem = pltpu.VMEM
    dma = pltpu.SemaphoreType.DMA
    pred, gin, gout, stat = pl.pallas_call(
        functools.partial(step_kernel, dp, mp, chunks),
        out_shape=[
            jax.ShapeDtypeStruct((rows, out_w), bf16),
            jax.ShapeDtypeStruct((units, in_w), f32),
            jax.ShapeDtypeStruct((units, out_w), f32),
            jax.ShapeDtypeStruct((8, 128), f32),
        ],
        in_specs=[pl.BlockSpec(memory_space=vmem)] * 4,
        out_specs=[pl.BlockSpec(memory_space=vmem)] * 4,
        scratch_shapes=[
            vmem((batch, in_w), bf16),
            vmem((batch, out_w), bf16),
            vmem((rows, out_w), bf16),
            vmem((mp, units, in_w), bf16),
            vmem((mp, units, out_w), bf16),
            vmem((batch, all_units), f32),
            vmem((batch, all_units), bf16),
            vmem((batch, out_w), f32),
            vmem((chips, rows, out_w), bf16),
            vmem((chips, rows, out_w), bf16),
            vmem((n_right, rows, out_w), bf16),
            vmem((n_right, rows, out_w), bf16),
            vmem((n_left, rows, out_w), bf16),
            vmem((n_left, rows, out_w), bf16),
            vmem((mp - 1, units, out_w), bf16),
            vmem((mp - 1, units, out_w), bf16),
            vmem((mp - 1, units, in_w), bf16),
            vmem((mp - 1, units, in_w), bf16),
            dma((2, 2, mp - 1)),
            dma((2, 3, chips, chunks)),
            dma((2, 3, chips, chunks)),
            dma((2, chips)),
            dma((2, n_right)),
            dma((2, n_left)),
            dma((2, 2, mp - 1)),
        ],
        compiler_params=pltpu.CompilerParams(collective_id=0, has_side_effects=True),
        name="step",
    )(features, targets, w_in, w_out)
    stats = lax.all_gather(stat[:2, :1], ("dp", "mp"), axis=1, tiled=True)
    totals = jnp.sum(stats, axis=1)
    count_params = units_real * mp * dp * (in_w + out_w)
    scale = lax.rsqrt(totals[1] / count_params + 1e-06)
    loss = totals[0] / (rows * mp * dp * out_w)
    return (pred, gin[:units_real] * scale, gout[:units_real] * scale, loss)


def solution(mesh):
    in_specs = (
        P(("dp", "mp"), None),
        P(("dp", "mp"), None),
        P(("dp", "mp"), None),
        P(("mp", "dp"), None),
        P(("mp", "dp"), None),
    )
    out_specs = (P(("dp", "mp"), None), P(("mp", "dp"), None), P(("mp", "dp"), None), P())
    return jax.shard_map(body, mesh=mesh, in_specs=in_specs, out_specs=out_specs, check_vma=False)
```

time: 403 us -> 145 us (0.36)
  waiting for transfers between devices: 292 us -> 0 us
  Pallas kernels: 0 us -> 69.4 us
  matrix products: 20.1 us -> 0 us
  between operations: 17.6 us -> 3.13 us
    reduce_scatter x2 -> x0, waiting for transfers between devices: 199 us -> none  [the longest x1 108 us: body(): lax.psum_scatter(left_product(preact_grad, features), 'dp', scatter_dimen...]
    all_gather x2 -> x0, waiting for transfers between devices: 91.7 us -> none  [the longest x1 47.4 us: body(): local_out = lax.all_gather(w_out, 'dp', axis=0, tiled=True)]
    pallas_call x0 -> x1, Pallas kernels: none -> 69.4 us  [body(): pl.pallas_call(functools.partial(step_kernel, dp, mp, chunks), out_shape=...]
    all_gather x3 -> x1, blocking collectives: 16 us -> 65.1 us  [body(): stats = lax.all_gather(stat[:2, :1], ('dp', 'mp'), axis=1, tiled=True)]
    psum x1 -> x0, blocking collectives: 40.5 us -> none  [body(): square_total = lax.psum(square_part, ('dp', 'mp'))]
    dot_general x4 -> x0, matrix products: 20.1 us -> none  [the longest x2 13.6 us: left_product(): lax.dot_general(left_side, right_side, (((0,), (0,)), ((), ())), preferre...]
    all_to_all x1 -> x0, blocking collectives: 7.25 us -> none  [body(): lax.all_to_all(stacked, 'mp', split_axis=0, concat_axis=0, tiled=True)]
    reduce_sum x5 -> x1, other arithmetic: 4.97 us -> 0.05 us  [body(): totals = jnp.sum(stats, axis=1)]
  transfers between devices with their start and end apart: 4 -> 0, of which waited for: 4 -> 0; matrix products, arithmetic and copies ran while one was open for 4% -> 0% of each run, Pallas kernels for 0% -> 0%
where the time goes in v1:
time: 145 us
  Pallas kernels  69.4 us (48%)
  blocking collectives  65.1 us (45%)
  other arithmetic  5.12 us (4%)
  between operations  3.13 us (2%)
  local copies, waits for them, and re-layouts  2.07 us (1%)
    pallas_call x1, Pallas kernels, body(): pl.pallas_call(functools.partial(step_kernel, dp, mp, chunks), out_shape=...  69.4 us
    all_gather x1, blocking collectives, body(): stats = lax.all_gather(stat[:2, :1], ('dp', 'mp'), axis=1, tiled=True)  65.1 us

profile of v1, /device:TPU:0, one launch (start us, length us, event | category | flops | bytes accessed | tf_op | source)
XLA Modules:
  0.0 144.9 jit_solution(8600311929370002688)
XLA Ops:
  0.6 0.8 fusion
  1.4 1.6 %pad_maximum_fusion.feat_ref = bf16[16,2704]{1,0:T(8,128)(2,1)} fusion(bf16[16,52]{1,0:T(8,128)(2,1)S(1)} %convert_element_type.3, bf16[16,2652]{1,0:T(8,128)(2,1)} %param.5), kind=kLoop, calls=%fused_computation.2 | loop fusion | flops 173056 | bytes 173056 | tf_op jit(solution)/shard_map/concatenate | solution.py:241
  3.0 69.4 %step.1 = (bf16[16,2652]{1,0:T(8,128)(2,1)}, f32[48,2704]{1,0:T(8,128)}, f32[48,2652]{1,0:T(8,128)}, f32[8,128]{1,0:T(8,128)}) custom-call(bf16[16,2704]{1,0:T(8,128)(2,1)} %pad_maximum_fusion.feat_ref, bf16[16,2652]{1,0:T(8,128)(2,1)} %targets_ref.1, bf16[48,2704]{1,0:T(8,128)(2,1)} %w_in_ref.1, bf16[48,2652]{1,0:T(8,128)(2,1)} %w_out_ref.1), custom_call_target="tpu_custom_call" | custom-call | tf_op jit(solution)/shard_map/step/pallas_call | solution.py:251
  72.5 0.8 slice_reduce_fusion
  73.3 0.0 copy-start
  73.3 65.1 %all-gather = f32[32,1,2]{2,1,0:T(1,128)S(1)} all-gather(f32[1,1,2]{2,1,0:T(1,128)S(1)} %bitcast.3), channel_id=1, replica_groups=mesh['dp'=16,'mp'=2] {'dp','mp'}, dimensions={0}, use_global_device_ids=true | all-gather | bytes 264 | tf_op jit(solution)/shard_map/all_gather | solution.py:291
  138.4 0.1 reduce_sum.9
  138.4 0.6 fusion.1
  140.4 1.9 %broadcast_multiply_fusion.1 = f32[48,2652]{1,0:T(8,128)} fusion(f32[48,2652]{1,0:T(8,128)} %get-tuple-element.11, f32[]{:T(128)} %bitcast), kind=kLoop, calls=%fused_computation.1 | loop fusion | flops 127296 | bytes 1018372 | tf_op jit(solution)/shard_map/mul | solution.py:296
  142.2 0.0 copy-done
  142.2 0.0 copy-start.1
  142.2 0.8 broadcast_multiply_fusion
  143.1 0.1 copy-done.1
  143.1 0.6 copy.13
  (1 shorter events, 0.0 us)
Async XLA Ops:
  73.3 69.0 %copy-start = (f32[48,2704]{1,0:T(8,128)S(1)}, f32[48,2704]{1,0:T(8,128)}, u32[]{:S(2)}) copy-start(f32[48,2704]{1,0:T(8,128)} %get-tuple-element.9) | copy-start | bytes 1557508
  142.2 0.9 copy-start.1

commit v2 on v1

v2 whole, which is shorter than its diff:
```python
import functools

import jax
import jax.numpy as jnp
from jax import lax
from jax.experimental import pallas as pl
from jax.experimental.pallas import tpu as pltpu
from jax.sharding import PartitionSpec as P

CARDS = 52
MESH = pl.DeviceIdType.MESH
GELU_K = 0.7978845608028654
GELU_C = 0.044715


def huber_terms(error_value):
    magnitude = jnp.abs(error_value)
    return jnp.where(magnitude <= 1.0, 0.5 * error_value * error_value, magnitude - 0.5)


def dot_nt(a, b):
    return lax.dot_general(a, b, (((1,), (1,)), ((), ())), preferred_element_type=jnp.float32)


def dot_nn(a, b):
    return lax.dot_general(a, b, (((1,), (0,)), ((), ())), preferred_element_type=jnp.float32)


def column_chunks(width, count):
    tiles = -(-width // 128)
    edges = [min(width, 128 * (-(-tiles * k // count))) for k in range(count + 1)]
    return [pl.ds(a, b - a) for a, b in zip(edges[:-1], edges[1:]) if b > a]


def dot_tn(a, b):
    return lax.dot_general(a, b, (((0,), (0,)), ((), ())), preferred_element_type=jnp.float32)


def step_kernel(
    dp, mp, chunks, count_params, count_values,
    ranges_ref, board_ref, targets_ref, w_in_ref, w_out_ref,
    pred_ref, gin_ref, gout_ref, stat_ref,
    feat_own, feats, ogs, og_own, win, wout, preact, hidden, partial, go_acc, gi_acc,
    sp, lp, sr, rr, sl, rl, sgo, lgo, sgi, lgi, st, ld1, st2, ld2,
    w_sem, ag1, ag2, p_sem, r_sem, l_sem, g_sem, s1_sem, s2_sem,
):
    chips = dp // 2
    steps = chips // 2
    rows = ranges_ref.shape[0]
    units = w_in_ref.shape[0]
    me = lax.axis_index("dp")
    me_mp = lax.axis_index("mp")
    core = me % 2
    chip = me // 2
    odd = chip % 2
    pos = (1 - odd) * (chip // 2) + odd * (chips - 1 - chip // 2)

    def at(rel):
        there = (pos + rel + chips) % chips
        half = there // (chips // 2)
        where = (1 - half) * (2 * there) + half * (2 * (chips - 1 - there) + 1)
        return (where * 2 + core, me_mp)

    right, left = at(1), at(-1)
    partner = (chip * 2 + 1 - core, me_mp)
    peers = [(me, (me_mp + j) % mp) for j in range(1, mp)]
    back_peers = [(me, (me_mp - j + mp) % mp) for j in range(1, mp)]
    line = [at(r) for r in range(1, chips)]
    square = [
        (chip * 2 + (core + c) % 2, (me_mp + j) % mp)
        for c in range(2) for j in range(mp) if c or j
    ]

    barrier = pltpu.get_barrier_semaphore()
    for other in line + square:
        pl.semaphore_signal(barrier, inc=1, device_id=other, device_id_type=MESH)

    cards = lax.broadcasted_iota(jnp.int32, (rows, CARDS), 1)
    onehot = jnp.zeros((rows, CARDS), jnp.float32)
    for k in range(board_ref.shape[1]):
        onehot = onehot + (board_ref[:, k:k + 1] == cards).astype(jnp.float32)
    feat_own[...] = jnp.concatenate(
        [ranges_ref[...].astype(jnp.float32), onehot], axis=1
    ).astype(jnp.bfloat16)
    pl.semaphore_wait(barrier, len(line + square))

    def send(src, dst, sems, index, device):
        copy = pltpu.make_async_remote_copy(
            src_ref=src, dst_ref=dst,
            send_sem=sems.at[(0,) + index], recv_sem=sems.at[(1,) + index],
            device_id=device, device_id_type=MESH,
        )
        copy.start()
        return copy

    def spot(slot, side):
        return pl.ds((2 * slot + side) * rows, rows)

    def half_of(side, count):
        return range(count // 2) if side == 0 else range(count // 2, count)

    def start_gather(own_ref, buf, sems):
        pieces = column_chunks(buf.shape[1], chunks)
        flying = {}
        last = steps == 1
        for k, piece in enumerate(pieces):
            for side, device in ((0, right), (1, left)):
                if last and k not in half_of(side, len(pieces)):
                    continue
                slot = 1 if last else 1 + side
                flying[side, k] = send(
                    own_ref.at[:, piece], buf.at[spot(slot, 0), piece], sems, (side, 0, k), device
                )
        own = [
            send(own_ref.at[:, piece], buf.at[spot(0, 1), piece], sems, (2, 0, k), partner)
            for k, piece in enumerate(pieces)
        ]
        return flying, own

    def finish_gather(own_ref, buf, sems, started, before_last):
        pieces = column_chunks(buf.shape[1], chunks)
        flying, partner_copies = started
        buf[spot(0, 0), :] = own_ref[...]
        done = []
        by_slot = {0: list(partner_copies)}
        for s in range(steps):
            coming = {}
            final, next_final = s == steps - 1, s == steps - 2
            for k, piece in enumerate(pieces):
                for side, device in ((0, right), (1, left)):
                    if (side, k) not in flying:
                        continue
                    copy = flying[side, k]
                    copy.wait_recv()
                    done.append(copy)
                    slot = 2 * s + 1 if final else 2 * s + 1 + side
                    part = buf.at[spot(slot, 0), piece]
                    if not final and not (next_final and k not in half_of(side, len(pieces))):
                        target = 2 * s + 3 if next_final else 2 * s + 3 + side
                        coming[side, k] = send(
                            part, buf.at[spot(target, 0), piece], sems, (side, s + 1, k), device
                        )
                    by_slot.setdefault(slot, []).append(
                        send(part, buf.at[spot(slot, 1), piece], sems, (2, slot, k), partner)
                    )
            flying = coming
            if next_final:
                for slot in range(chips - 1):
                    for copy in by_slot[slot]:
                        copy.wait_recv()
                before_last()
        for copy in by_slot[chips - 1]:
            copy.wait_recv()
        for copy in done + [c for cs in by_slot.values() for c in cs]:
            copy.wait_send()

    started = start_gather(feat_own, feats, ag1)
    in_copies = [
        send(w_in_ref, win.at[j + 1], w_sem, (0, j), device) for j, device in enumerate(back_peers)
    ]
    out_copies = [
        send(w_out_ref, wout.at[j + 1], w_sem, (1, j), device) for j, device in enumerate(back_peers)
    ]
    win[0] = w_in_ref[...]
    wout[0] = w_out_ref[...]
    all_units = mp * units
    batch = dp * rows
    split = 2 * rows * (chips - 1)
    middle = batch // 2

    def hidden_rows(a, b):
        pre = dot_nt(feats[a:b, :], win[...].reshape(all_units, win.shape[2]))
        preact[a:b, :] = pre
        tanh_value = jnp.tanh(GELU_K * (pre + GELU_C * pre * pre * pre))
        hidden[a:b, :] = (0.5 * pre * (1.0 + tanh_value)).astype(jnp.bfloat16)

    def early_hidden():
        for copy in in_copies:
            copy.wait()
        hidden_rows(0, split)

    finish_gather(feat_own, feats, ag1, started, early_hidden)
    hidden_rows(split, batch)
    for copy in out_copies:
        copy.wait()
    shared = {}
    for a, b in ((middle, batch), (0, middle)):
        partial[a:b, :] = dot_nn(hidden[a:b, :], wout[...].reshape(all_units, wout.shape[2]))
        for slot in reversed(range(a // (2 * rows), b // (2 * rows))):
            sp[slot] = partial[spot(slot, 1), :].astype(jnp.bfloat16)
            shared[slot] = send(sp.at[slot], lp.at[slot], p_sem, (slot,), partner)

    pieces = column_chunks(partial.shape[1], chunks)

    def contribution(slot, piece):
        return partial[spot(slot, 0), piece] + lp[slot, :, piece].astype(jnp.float32)

    sums = {}
    sides = ((0, sr, rr, r_sem, right), (1, sl, rl, l_sem, left))
    waited = set()
    for s in range(steps):
        for k, piece in enumerate(pieces):
            for side, outgoing, landed, sems, device in sides:
                if s == 0 and k not in half_of(side, len(pieces)):
                    continue
                distance = steps - s
                slot = chips - 1 if s == 0 else (2 * distance if side == 0 else 2 * distance - 1)
                if slot not in waited:
                    shared[slot].wait_recv()
                    waited.add(slot)
                total = contribution(slot, piece)
                if (side, s - 1, k) in sums:
                    sums[side, s - 1, k].wait_recv()
                    total = total + landed[s - 1, :, piece].astype(jnp.float32)
                outgoing[s, :, piece] = total.astype(jnp.bfloat16)
                sums[side, s, k] = send(
                    outgoing.at[s, :, piece], landed.at[s, :, piece], sems, (s, k), device
                )
    shared[0].wait_recv()
    loss_part = 0.0
    for k, piece in enumerate(pieces):
        total = contribution(0, piece)
        for side, outgoing, landed, sems, device in sides:
            if (side, steps - 1, k) in sums:
                sums[side, steps - 1, k].wait_recv()
                total = total + landed[steps - 1, :, piece].astype(jnp.float32)
        pred_ref[:, piece] = total.astype(jnp.bfloat16)
        error_value = total - targets_ref[:, piece].astype(jnp.float32)
        og_own[:, piece] = jnp.clip(error_value, -1.0, 1.0).astype(jnp.bfloat16)
        loss_part = loss_part + jnp.sum(huber_terms(error_value))
    started = start_gather(og_own, ogs, ag2)
    pre = preact[...]
    tanh_value = jnp.tanh(GELU_K * (pre + GELU_C * pre * pre * pre))
    preact[...] = 0.5 * (1.0 + tanh_value) + 0.5 * pre * (1.0 - tanh_value * tanh_value) * (
        GELU_K * (1.0 + 3.0 * GELU_C * pre * pre)
    )
    for copy in list(shared.values()) + list(sums.values()):
        copy.wait_send()

    def early_grads():
        back = dot_nt(ogs[:split, :], wout[...].reshape(all_units, wout.shape[2]))
        pre_grad = (back * preact[:split, :]).astype(jnp.bfloat16)
        go_acc[...] = dot_tn(hidden[:split, :], ogs[:split, :])
        gi_acc[...] = dot_tn(pre_grad, feats[:split, :])

    finish_gather(og_own, ogs, ag2, started, early_grads)

    grad_copies = []

    def ship(acc, late, staged, landed, lane, out_ref):
        for j, device in enumerate(peers):
            mine = slice((j + 1) * units, (j + 2) * units)
            staged[j] = (acc[mine, :] + late[mine, :]).astype(jnp.bfloat16)
            grad_copies.append(send(staged.at[j], landed.at[j], g_sem, (lane, j), device))
        out_ref[...] = acc[:units, :] + late[:units, :]

    ship(go_acc, dot_tn(hidden[split:, :], ogs[split:, :]), sgo, lgo, 0, gout_ref)
    back = dot_nt(ogs[split:, :], wout[...].reshape(all_units, wout.shape[2]))
    pre_grad = (back * preact[split:, :]).astype(jnp.bfloat16)
    ship(gi_acc, dot_tn(pre_grad, feats[split:, :]), sgi, lgi, 1, gin_ref)

    def own_total(out_ref, landed, lane):
        for copy in grad_copies[lane * (mp - 1):(lane + 1) * (mp - 1)]:
            copy.wait()
        total = out_ref[...]
        for j in range(mp - 1):
            total = total + landed[j].astype(jnp.float32)
        out_ref[...] = total
        return jnp.sum(total * total)

    squares = own_total(gout_ref, lgo, 0)
    squares = squares + own_total(gin_ref, lgi, 1)
    row = lax.broadcasted_iota(jnp.int32, stat_ref.shape, 0)
    st[...] = jnp.where(row == 0, loss_part, squares)
    copies = [
        send(st, ld1.at[r], s1_sem, (r,), device) for r, device in enumerate(line)
    ]
    total = st[...]
    for r, copy in enumerate(copies):
        copy.wait()
        total = total + ld1[r]
    st2[...] = total
    copies = [
        send(st2, ld2.at[r], s2_sem, (r,), device) for r, device in enumerate(square)
    ]
    for r, copy in enumerate(copies):
        copy.wait()
        total = total + ld2[r]
    stat_ref[...] = jnp.where(
        row == 0, total / count_values, lax.rsqrt(total / count_params + 1e-06)
    )


def body(ranges, board, targets, w_in, w_out):
    mp = lax.axis_size("mp")
    dp = lax.axis_size("dp")
    rows, out_w = targets.shape
    units_real, in_w = w_in.shape
    pad = -units_real % 16
    if pad:
        w_in = jnp.pad(w_in, ((0, pad), (0, 0)))
        w_out = jnp.pad(w_out, ((0, pad), (0, 0)))
    units = units_real + pad
    chips = dp // 2
    steps = chips // 2
    chunks = 4
    batch = dp * rows
    all_units = mp * units
    bf16, f32 = jnp.bfloat16, jnp.float32
    vmem = pltpu.VMEM
    dma = pltpu.SemaphoreType.DMA
    count_params = units_real * mp * dp * (in_w + out_w)
    count_values = rows * mp * dp * out_w
    pred, gin, gout, stat = pl.pallas_call(
        functools.partial(step_kernel, dp, mp, chunks, count_params, count_values),
        out_shape=[
            jax.ShapeDtypeStruct((rows, out_w), bf16),
            jax.ShapeDtypeStruct((units, in_w), f32),
            jax.ShapeDtypeStruct((units, out_w), f32),
            jax.ShapeDtypeStruct((8, 128), f32),
        ],
        in_specs=[pl.BlockSpec(memory_space=vmem)] * 5,
        out_specs=[pl.BlockSpec(memory_space=vmem)] * 4,
        scratch_shapes=[
            vmem((rows, in_w), bf16),
            vmem((batch, in_w), bf16),
            vmem((batch, out_w), bf16),
            vmem((rows, out_w), bf16),
            vmem((mp, units, in_w), bf16),
            vmem((mp, units, out_w), bf16),
            vmem((batch, all_units), f32),
            vmem((batch, all_units), bf16),
            vmem((batch, out_w), f32),
            vmem((all_units, out_w), f32),
            vmem((all_units, in_w), f32),
            vmem((chips, rows, out_w), bf16),
            vmem((chips, rows, out_w), bf16),
            vmem((steps, rows, out_w), bf16),
            vmem((steps, rows, out_w), bf16),
            vmem((steps, rows, out_w), bf16),
            vmem((steps, rows, out_w), bf16),
            vmem((mp - 1, units, out_w), bf16),
            vmem((mp - 1, units, out_w), bf16),
            vmem((mp - 1, units, in_w), bf16),
            vmem((mp - 1, units, in_w), bf16),
            vmem((8, 128), f32),
            vmem((chips - 1, 8, 128), f32),
            vmem((8, 128), f32),
            vmem((2 * mp - 1, 8, 128), f32),
            dma((2, 2, mp - 1)),
            dma((2, 3, chips, chunks)),
            dma((2, 3, chips, chunks)),
            dma((2, chips)),
            dma((2, steps, chunks)),
            dma((2, steps, chunks)),
            dma((2, 2, mp - 1)),
            dma((2, chips - 1)),
            dma((2, 2 * mp - 1)),
        ],
        compiler_params=pltpu.CompilerParams(collective_id=0, has_side_effects=True),
        name="step",
    )(ranges, board, targets, w_in, w_out)
    scale = stat[1:2, :1]
    return (pred, gin[:units_real] * scale, gout[:units_real] * scale, stat[0, 0])


def solution(mesh):
    in_specs = (
        P(("dp", "mp"), None),
        P(("dp", "mp"), None),
        P(("dp", "mp"), None),
        P(("mp", "dp"), None),
        P(("mp", "dp"), None),
    )
    out_specs = (P(("dp", "mp"), None), P(("mp", "dp"), None), P(("mp", "dp"), None), P())
    return jax.shard_map(body, mesh=mesh, in_specs=in_specs, out_specs=out_specs, check_vma=False)
```

time: 145 us -> 84.2 us (0.58)
  blocking collectives: 65.1 us -> 0 us
  Pallas kernels: 69.4 us -> 76 us
  between operations: 3.13 us -> 0.65 us
    all_gather x1 -> x0, blocking collectives: 65.1 us -> none  [body(): stats = lax.all_gather(stat[:2, :1], ('dp', 'mp'), axis=1, tiled=True)]
    pallas_call x1, Pallas kernels: 69.4 us -> 76 us  [body(): pl.pallas_call(functools.partial(step_kernel, dp, mp, chunks, count_param...]
    concatenate x1 -> x0, other arithmetic: 1.61 us -> none  [body(): features = jnp.concatenate([ranges, onehot], axis=1)]
where the time goes in v2:
time: 84.2 us; the launch traced here: 83.9 us
  Pallas kernels  76 us (90%)
  other arithmetic  4.02 us (5%)
  local copies, waits for them, and re-layouts  3.28 us (4%)
    pallas_call x1, Pallas kernels, body(): pl.pallas_call(functools.partial(step_kernel, dp, mp, chunks, count_param...  76 us
    mul x1, other arithmetic, body(): gout[:units_real] * scale  2.5 us
    unnamed x6, local copies, waits for them, and re-layouts  2.01 us

profile of v2, /device:TPU:0, one launch (start us, length us, event | category | flops | bytes accessed | tf_op | source)
XLA Modules:
  0.0 83.9 jit_solution(3710736531671533097)
XLA Ops:
  0.6 1.4 %copy.9.board_ref = s32[16,5]{1,0:T(8,128)} copy(s32[16,5]{0,1:T(8,128)} %param.6) | data formatting | bytes 640 | tf_op args[1]
  2.0 76.0 %step.1 = (bf16[16,2652]{1,0:T(8,128)(2,1)}, f32[48,2704]{1,0:T(8,128)}, f32[48,2652]{1,0:T(8,128)}, f32[8,128]{1,0:T(8,128)}) custom-call(bf16[16,2652]{1,0:T(8,128)(2,1)} %ranges_ref.1, s32[16,5]{1,0:T(8,128)} %copy.9.board_ref, bf16[16,2652]{1,0:T(8,128)(2,1)} %targets_ref.1, bf16[48,2704]{1,0:T(8,128)(2,1)} %w_in_ref.1, bf16[48,2652]{1,0:T(8,128)(2,1)} %w_out_ref.1), custom_call_target="tpu_custom_call" | custom-call | tf_op jit(solution)/shard_map/step/pallas_call | solution.py:314
  78.0 0.0 copy-start
  78.0 1.3 %fusion = (f32[1,1]{1,0:T(1,128)}, f32[1,1]{1,0:T(1,128)}) fusion(f32[8,128]{1,0:T(8,128)} %get-tuple-element.10), kind=kLoop, calls=%fused_computation.2 | loop fusion | bytes 16 | tf_op jit(solution)/shard_map/slice | solution.py:364
  79.2 2.5 %broadcast_multiply_fusion.1 = f32[48,2652]{1,0:T(8,128)} fusion(f32[48,2652]{1,0:T(8,128)} %get-tuple-element.11, f32[]{:T(128)} %bitcast), kind=kLoop, calls=%fused_computation.1 | loop fusion | flops 127296 | bytes 1018372 | tf_op jit(solution)/shard_map/mul | solution.py:364
  81.7 0.0 copy-done
  81.7 0.0 copy-start.1
  81.7 1.5 %broadcast_multiply_fusion = f32[48,2704]{1,0:T(8,128)} fusion(f32[48,2704]{1,0:T(8,128)S(1)} %copy-done, f32[]{:T(128)} %bitcast), kind=kLoop, calls=%fused_computation | loop fusion | flops 129792 | bytes 1038340 | tf_op jit(solution)/shard_map/mul | solution.py:364
  83.3 0.0 copy-done.1
  83.3 0.6 copy.11
Async XLA Ops:
  78.0 3.8 %copy-start = (f32[48,2704]{1,0:T(8,128)S(1)}, f32[48,2704]{1,0:T(8,128)}, u32[]{:S(2)}) copy-start(f32[48,2704]{1,0:T(8,128)} %get-tuple-element.9) | copy-start | bytes 1557508
  81.7 1.5 %copy-start.1 = (bf16[16,2652]{1,0:T(8,128)(2,1)S(1)}, bf16[16,2652]{1,0:T(8,128)(2,1)}, u32[]{:S(2)}) copy-start(bf16[16,2652]{1,0:T(8,128)(2,1)} %get-tuple-element.18) | copy-start | bytes 254596

commit v3 on v2

--- a/solution.py
+++ b/solution.py
@@ -37,12 +37,12 @@
 
 
 def step_kernel(
-    dp, mp, chunks, count_params, count_values,
+    dp, mp, chunks, swap, count_params, count_values,
     ranges_ref, board_ref, targets_ref, w_in_ref, w_out_ref,
     pred_ref, gin_ref, gout_ref, stat_ref,
     feat_own, feats, ogs, og_own, win, wout, preact, hidden, partial, go_acc, gi_acc,
-    sp, lp, sr, rr, sl, rl, sgo, lgo, sgi, lgi, st, ld1, st2, ld2,
-    w_sem, ag1, ag2, p_sem, r_sem, l_sem, g_sem, s1_sem, s2_sem,
+    sp, lp, sr, rr, sl, rl, sgo, lgo, sgi, lgi, st, ld1, st2, ld2, pf, spg, lpg,
+    w_sem, ag1, ag2, p_sem, r_sem, l_sem, g_sem, s1_sem, s2_sem, f_sem, pg_sem,
 ):
     chips = dp // 2
     steps = chips // 2
@@ -75,12 +75,12 @@
     for other in line + square:
         pl.semaphore_signal(barrier, inc=1, device_id=other, device_id_type=MESH)
 
-    cards = lax.broadcasted_iota(jnp.int32, (rows, CARDS), 1)
-    onehot = jnp.zeros((rows, CARDS), jnp.float32)
-    for k in range(board_ref.shape[1]):
-        onehot = onehot + (board_ref[:, k:k + 1] == cards).astype(jnp.float32)
+    cards = lax.broadcasted_iota(jnp.int32, (CARDS, rows), 0)
+    onehot = jnp.zeros((CARDS, rows), jnp.float32)
+    for k in range(board_ref.shape[0]):
+        onehot = onehot + (board_ref[k:k + 1, :] == cards).astype(jnp.float32)
     feat_own[...] = jnp.concatenate(
-        [ranges_ref[...].astype(jnp.float32), onehot], axis=1
+        [ranges_ref[...].astype(jnp.float32), jnp.transpose(onehot)], axis=1
     ).astype(jnp.bfloat16)
     pl.semaphore_wait(barrier, len(line + square))
 
@@ -180,6 +180,11 @@
         hidden_rows(0, split)
 
     finish_gather(feat_own, feats, ag1, started, early_hidden)
+    feat_copies = []
+    if swap:
+        feat_copies = [
+            send(feats, pf.at[j], f_sem, (j,), device) for j, device in enumerate(peers)
+        ]
     hidden_rows(split, batch)
     for copy in out_copies:
         copy.wait()
@@ -237,11 +242,24 @@
     for copy in list(shared.values()) + list(sums.values()):
         copy.wait_send()
 
+    pg_copies = []
+
+    def swap_pre_grad(pre_grad, lane, a, b):
+        for j, device in enumerate(peers):
+            spg[j, a:b, :] = pre_grad[:, (j + 1) * units:(j + 2) * units]
+            pg_copies.append(send(
+                spg.at[j, pl.ds(a, b - a)], lpg.at[j, pl.ds(a, b - a)], pg_sem, (lane, j), device
+            ))
+
     def early_grads():
         back = dot_nt(ogs[:split, :], wout[...].reshape(all_units, wout.shape[2]))
         pre_grad = (back * preact[:split, :]).astype(jnp.bfloat16)
         go_acc[...] = dot_tn(hidden[:split, :], ogs[:split, :])
-        gi_acc[...] = dot_tn(pre_grad, feats[:split, :])
+        if swap:
+            gin_ref[...] = dot_tn(pre_grad[:, :units], feats[:split, :])
+            swap_pre_grad(pre_grad, 0, 0, split)
+        else:
+            gi_acc[...] = dot_tn(pre_grad, feats[:split, :])
 
     finish_gather(og_own, ogs, ag2, started, early_grads)
 
@@ -254,10 +272,21 @@
             grad_copies.append(send(staged.at[j], landed.at[j], g_sem, (lane, j), device))
         out_ref[...] = acc[:units, :] + late[:units, :]
 
-    ship(go_acc, dot_tn(hidden[split:, :], ogs[split:, :]), sgo, lgo, 0, gout_ref)
+    if not swap:
+        ship(go_acc, dot_tn(hidden[split:, :], ogs[split:, :]), sgo, lgo, 0, gout_ref)
     back = dot_nt(ogs[split:, :], wout[...].reshape(all_units, wout.shape[2]))
     pre_grad = (back * preact[split:, :]).astype(jnp.bfloat16)
-    ship(gi_acc, dot_tn(pre_grad, feats[split:, :]), sgi, lgi, 1, gin_ref)
+    if swap:
+        swap_pre_grad(pre_grad, 1, split, batch)
+        ship(go_acc, dot_tn(hidden[split:, :], ogs[split:, :]), sgo, lgo, 0, gout_ref)
+        gin_ref[...] = gin_ref[...] + dot_tn(pre_grad[:, :units], feats[split:, :])
+        for copy in feat_copies + pg_copies:
+            copy.wait()
+        for j in range(mp - 1):
+            gin_ref[...] = gin_ref[...] + dot_tn(lpg[j], pf[j])
+        squares = jnp.sum(gin_ref[...] * gin_ref[...])
+    else:
+        ship(gi_acc, dot_tn(pre_grad, feats[split:, :]), sgi, lgi, 1, gin_ref)
 
     def own_total(out_ref, landed, lane):
         for copy in grad_copies[lane * (mp - 1):(lane + 1) * (mp - 1)]:
@@ -268,9 +297,10 @@
         out_ref[...] = total
         return jnp.sum(total * total)
 
-    squares = own_total(gout_ref, lgo, 0)
-    squares = squares + own_total(gin_ref, lgi, 1)
-    row = lax.broadcasted_iota(jnp.int32, stat_ref.shape, 0)
+    if not swap:
+        squares = own_total(gin_ref, lgi, 1)
+    squares = squares + own_total(gout_ref, lgo, 0)
+    row = lax.broadcasted_iota(jnp.int32, st.shape, 0)
     st[...] = jnp.where(row == 0, loss_part, squares)
     copies = [
         send(st, ld1.at[r], s1_sem, (r,), device) for r, device in enumerate(line)
@@ -286,9 +316,10 @@
     for r, copy in enumerate(copies):
         copy.wait()
         total = total + ld2[r]
-    stat_ref[...] = jnp.where(
-        row == 0, total / count_values, lax.rsqrt(total / count_params + 1e-06)
-    )
+    stat_ref[...] = total[0:1, 0:1] / count_values
+    scale = lax.rsqrt(total[1:2, 0:1] / count_params + 1e-06)
+    gout_ref[...] = gout_ref[...] * scale
+    gin_ref[...] = gin_ref[...] * scale
 
 
 def body(ranges, board, targets, w_in, w_out):
@@ -304,6 +335,7 @@
     chips = dp // 2
     steps = chips // 2
     chunks = 4
+    swap = (mp - 1) * dp * rows * in_w * 2 <= 8 * 2**20
     batch = dp * rows
     all_units = mp * units
     bf16, f32 = jnp.bfloat16, jnp.float32
@@ -312,12 +344,12 @@
     count_params = units_real * mp * dp * (in_w + out_w)
     count_values = rows * mp * dp * out_w
     pred, gin, gout, stat = pl.pallas_call(
-        functools.partial(step_kernel, dp, mp, chunks, count_params, count_values),
+        functools.partial(step_kernel, dp, mp, chunks, swap, count_params, count_values),
         out_shape=[
             jax.ShapeDtypeStruct((rows, out_w), bf16),
             jax.ShapeDtypeStruct((units, in_w), f32),
             jax.ShapeDtypeStruct((units, out_w), f32),
-            jax.ShapeDtypeStruct((8, 128), f32),
+            jax.ShapeDtypeStruct((1, 1), f32),
         ],
         in_specs=[pl.BlockSpec(memory_space=vmem)] * 5,
         out_specs=[pl.BlockSpec(memory_space=vmem)] * 4,
@@ -347,6 +379,9 @@
             vmem((chips - 1, 8, 128), f32),
             vmem((8, 128), f32),
             vmem((2 * mp - 1, 8, 128), f32),
+            vmem((mp - 1, batch, in_w) if swap else (1, 8, 128), bf16),
+            vmem((mp - 1, batch, units) if swap else (1, 8, 128), bf16),
+            vmem((mp - 1, batch, units) if swap else (1, 8, 128), bf16),
             dma((2, 2, mp - 1)),
             dma((2, 3, chips, chunks)),
             dma((2, 3, chips, chunks)),
@@ -356,12 +391,15 @@
             dma((2, 2, mp - 1)),
             dma((2, chips - 1)),
             dma((2, 2 * mp - 1)),
+            dma((2, mp - 1)),
+            dma((2, 2, mp - 1)),
         ],
         compiler_params=pltpu.CompilerParams(collective_id=0, has_side_effects=True),
         name="step",
-    )(ranges, board, targets, w_in, w_out)
-    scale = stat[1:2, :1]
-    return (pred, gin[:units_real] * scale, gout[:units_real] * scale, stat[0, 0])
+    )(ranges, board.T, targets, w_in, w_out)
+    if pad:
+        gin, gout = gin[:units_real], gout[:units_real]
+    return (pred, gin, gout, stat.reshape(()))
 
 
 def solution(mesh):

time: 84.2 us -> 80.4 us (0.955)
  other arithmetic: 4.02 us -> 0 us
  Pallas kernels: 76 us -> 73.5 us
  between operations: 0.65 us -> 2.39 us
  local copies, waits for them, and re-layouts: 3.28 us -> 4.26 us
    mul x2 -> x0, other arithmetic: 4.02 us -> none  [the longest x1 2.5 us: body(): gout[:units_real] * scale]
    pallas_call x1, Pallas kernels: 76 us -> 73.5 us  [body(): pl.pallas_call(functools.partial(step_kernel, dp, mp, chunks, swap, count...]
    unnamed x6 -> x5, local copies, waits for them, and re-layouts: 2.01 us -> 4.26 us
    slice x1 -> x0, local copies, waits for them, and re-layouts: 1.27 us -> none  [body(): stat[0, 0]]
where the time goes in v3:
time: 80.4 us; the launch traced here: 80.1 us
  Pallas kernels  73.5 us (91%)
  local copies, waits for them, and re-layouts  4.26 us (5%)
  between operations  2.39 us (3%)
    pallas_call x1, Pallas kernels, body(): pl.pallas_call(functools.partial(step_kernel, dp, mp, chunks, swap, count...  73.5 us
    unnamed x5, local copies, waits for them, and re-layouts  4.26 us

profile of v3, /device:TPU:0, one launch (start us, length us, event | category | flops | bytes accessed | tf_op | source)
XLA Modules:
  0.0 80.1 jit_solution(4806342011736642260)
XLA Ops:
  0.6 73.5 %step.1 = (bf16[16,2652]{1,0:T(8,128)(2,1)}, f32[48,2704]{1,0:T(8,128)}, f32[48,2652]{1,0:T(8,128)}, f32[1,1]{1,0:T(1,128)}) custom-call(bf16[16,2652]{1,0:T(8,128)(2,1)} %ranges_ref.1, s32[5,16]{1,0:T(8,128)} %bitcast.2, bf16[16,2652]{1,0:T(8,128)(2,1)} %targets_ref.1, bf16[48,2704]{1,0:T(8,128)(2,1)} %w_in_ref.1, bf16[48,2652]{1,0:T(8,128)(2,1)} %w_out_ref.1), custom_call_target="tpu_custom_call" | custom-call | tf_op jit(solution)/shard_map/step/pallas_call | solution.py:346
  74.1 1.5 %copy.13 = bf16[16,2652]{1,0:T(8,128)(2,1)} copy(bf16[16,2652]{1,0:T(8,128)(2,1)} %get-tuple-element.16) | data formatting | bytes 169728
  75.7 0.0 copy-start
  75.7 1.9 %copy.14 = f32[48,2704]{1,0:T(8,128)} copy(f32[48,2704]{1,0:T(8,128)} %get-tuple-element.17) | data formatting | bytes 1038336
  77.6 0.0 copy-done
  77.6 0.8 copy.15
Async XLA Ops:
  75.7 1.9 %copy-start = (f32[48,2652]{1,0:T(8,128)S(1)}, f32[48,2652]{1,0:T(8,128)}, u32[]{:S(2)}) copy-start(f32[48,2652]{1,0:T(8,128)} %get-tuple-element.18) | copy-start | bytes 1527556

commit v4 on v3

--- a/solution.py
+++ b/solution.py
@@ -334,7 +334,7 @@
     units = units_real + pad
     chips = dp // 2
     steps = chips // 2
-    chunks = 4
+    chunks = 2
     swap = (mp - 1) * dp * rows * in_w * 2 <= 8 * 2**20
     batch = dp * rows
     all_units = mp * units

time: 80.4 us -> 79 us (0.983)
  Pallas kernels: 73.5 us -> 72.1 us
    pallas_call x1, Pallas kernels: 73.5 us -> 72.1 us  [body(): pl.pallas_call(functools.partial(step_kernel, dp, mp, chunks, swap, count...]
where the time goes in v4:
time: 79 us; the launch traced here: 78.8 us
  Pallas kernels  72.1 us (91%)
  local copies, waits for them, and re-layouts  4.26 us (5%)
  between operations  2.39 us (3%)
    pallas_call x1, Pallas kernels, body(): pl.pallas_call(functools.partial(step_kernel, dp, mp, chunks, swap, count...  72.1 us
    unnamed x5, local copies, waits for them, and re-layouts  4.26 us

profile of v4, /device:TPU:0, one launch (start us, length us, event | category | flops | bytes accessed | tf_op | source)
XLA Modules:
  0.0 78.8 jit_solution(15498206478652050725)
XLA Ops:
  0.6 72.1 %step.1 = (bf16[16,2652]{1,0:T(8,128)(2,1)}, f32[48,2704]{1,0:T(8,128)}, f32[48,2652]{1,0:T(8,128)}, f32[1,1]{1,0:T(1,128)}) custom-call(bf16[16,2652]{1,0:T(8,128)(2,1)} %ranges_ref.1, s32[5,16]{1,0:T(8,128)} %bitcast.2, bf16[16,2652]{1,0:T(8,128)(2,1)} %targets_ref.1, bf16[48,2704]{1,0:T(8,128)(2,1)} %w_in_ref.1, bf16[48,2652]{1,0:T(8,128)(2,1)} %w_out_ref.1), custom_call_target="tpu_custom_call" | custom-call | tf_op jit(solution)/shard_map/step/pallas_call | solution.py:346
  72.8 1.5 %copy.13 = bf16[16,2652]{1,0:T(8,128)(2,1)} copy(bf16[16,2652]{1,0:T(8,128)(2,1)} %get-tuple-element.16) | data formatting | bytes 169728
  74.3 0.0 copy-start
  74.3 1.9 %copy.14 = f32[48,2704]{1,0:T(8,128)} copy(f32[48,2704]{1,0:T(8,128)} %get-tuple-element.17) | data formatting | bytes 1038336
  76.2 0.0 copy-done
  76.2 0.8 copy.15
Async XLA Ops:
  74.3 1.9 %copy-start = (f32[48,2652]{1,0:T(8,128)S(1)}, f32[48,2652]{1,0:T(8,128)}, u32[]{:S(2)}) copy-start(f32[48,2652]{1,0:T(8,128)} %get-tuple-element.18) | copy-start | bytes 1527556
